TPU v7x, 128 devices: a whole 4x4x4 slice. The times are simulated.
128 devices in a mesh: data: 64 (over z, y, x), model: 2 (over core).
Axes of the slice: x: 4, y: 4, z: 4, core: 2. Of those that a mesh axis runs over, the one named last changes fastest.
Arguments:
- x_teach: bfloat16 [256, 128, 768], P('data', 'model')
- x_stud: bfloat16 [256, 128, 312], P(('data', 'model'))
- t_up: bfloat16 [24, 768, 3072], P(None, None, 'model')
- t_down: bfloat16 [24, 3072, 768], P(None, 'model')
- t_gain: float32 [24, 768], replicated
- s_up: bfloat16 [6, 312, 1248], replicated
- s_down: bfloat16 [6, 1248, 312], replicated
- s_gain_mlp: float32 [6, 312], replicated
- s_gain_proj: float32 [6, 312], replicated
- s_proj: bfloat16 [6, 312, 768], replicated
Outputs:
- output 1: float32 [], replicated
- output 2: float32 [6, 312, 1248], replicated
- output 3: float32 [6, 1248, 312], replicated
- output 4: float32 [6, 312], replicated
- output 5: float32 [6, 312], replicated
- output 6: float32 [6, 312, 768], replicated
All inputs are finite; a program needn't handle non-finite values.
Results may differ from a plain program's by a relative error of at most 0.00403566.
Values are sent between devices in bfloat16 or wider.
A program may use at most 1 GiB of HBM per device.

v0:
```python
import functools
import jax
import jax.numpy as jnp
from jax import lax
from jax.sharding import PartitionSpec as P

NORM_EPS = 1e-6
gelu_tanh = functools.partial(jax.nn.gelu, approximate=True)


def rms_scale(values):
    widened = values.astype(jnp.float32)
    inv_rms = lax.rsqrt(jnp.mean(widened * widened, axis=-1, keepdims=True) + NORM_EPS)
    return widened, inv_rms


def rms_back(grad_unit, unit_vals, inv_rms):
    return inv_rms * (grad_unit - unit_vals * jnp.mean(grad_unit * unit_vals, axis=-1, keepdims=True))


def teacher_micro(hidden, up_loc, down_loc, gain_t, n_feat):
    per_feat = up_loc.shape[0] // n_feat
    feat_list = []
    for layer_idx in range(up_loc.shape[0]):
        widened, inv_rms = rms_scale(hidden)
        normed = (widened * inv_rms * gain_t[layer_idx]).astype(jnp.bfloat16)
        gathered = lax.all_gather(normed, 'model', axis=1, tiled=True)
        pre_act = jnp.einsum('bsd,df->bsf', gathered, up_loc[layer_idx], preferred_element_type=jnp.float32)
        hidden_act = gelu_tanh(pre_act).astype(jnp.bfloat16)
        part_out = jnp.einsum('bsf,fd->bsd', hidden_act, down_loc[layer_idx], preferred_element_type=jnp.float32).astype(jnp.bfloat16)
        reduced = lax.psum_scatter(part_out, 'model', scatter_dimension=1, tiled=True)
        hidden = (widened + reduced.astype(jnp.float32)).astype(jnp.bfloat16)
        if (layer_idx + 1) % per_feat == 0:
            feat_list.append(hidden)
    return feat_list


def feature_to_rows(feat_arr, model_n):
    rows_half = feat_arr.shape[0] // model_n
    grouped = feat_arr.reshape(model_n, rows_half, feat_arr.shape[1], feat_arr.shape[2])
    moved_rows = lax.all_to_all(grouped, 'model', 0, 2, tiled=True)
    return moved_rows.reshape(rows_half, feat_arr.shape[1] * model_n, feat_arr.shape[2])


def student_micro(x_rows, feat_list, up_s, down_s, gain_mlp, gain_proj, proj_s, loss_scale):
    n_layers = len(feat_list)
    stud_state = x_rows
    saved_acts = []
    loss_part = jnp.zeros((), jnp.float32)
    for layer_idx in range(n_layers):
        wide_in, inv_in = rms_scale(stud_state)
        unit_in = wide_in * inv_in
        normed = (unit_in * gain_mlp[layer_idx]).astype(jnp.bfloat16)
        pre_act = jnp.einsum('bsd,df->bsf', normed, up_s[layer_idx], preferred_element_type=jnp.float32)
        hidden_act = gelu_tanh(pre_act).astype(jnp.bfloat16)
        mlp_out = jnp.einsum('bsf,fd->bsd', hidden_act, down_s[layer_idx], preferred_element_type=jnp.float32)
        stud_state = (wide_in + mlp_out).astype(jnp.bfloat16)
        wide_out, inv_out = rms_scale(stud_state)
        unit_out = wide_out * inv_out
        projected = (unit_out * gain_proj[layer_idx]).astype(jnp.bfloat16)
        diff_err = jnp.einsum('bsd,dk->bsk', projected, proj_s[layer_idx], preferred_element_type=jnp.float32) - feat_list[layer_idx].astype(jnp.float32)
        loss_part = loss_part + jnp.sum(diff_err * diff_err) * loss_scale
        saved_acts.append((unit_in, inv_in, normed, pre_act, hidden_act, unit_out, inv_out, projected, diff_err))
    grad_state = jnp.zeros(x_rows.shape, jnp.float32)
    grad_lists = ([], [], [], [], [])
    for layer_idx in reversed(range(n_layers)):
        unit_in, inv_in, normed, pre_act, hidden_act, unit_out, inv_out, projected, diff_err = saved_acts[layer_idx]
        d_err = (2.0 * loss_scale * diff_err).astype(jnp.bfloat16)
        grad_proj = jnp.einsum('bsd,bsk->dk', projected, d_err, preferred_element_type=jnp.float32)
        d_projected = jnp.einsum('bsk,dk->bsd', d_err, proj_s[layer_idx], preferred_element_type=jnp.float32)
        grad_gain_proj = jnp.sum(d_projected * unit_out, axis=(0, 1))
        grad_state = grad_state + rms_back(d_projected * gain_proj[layer_idx], unit_out, inv_out)
        d_state = grad_state.astype(jnp.bfloat16)
        grad_down = jnp.einsum('bsf,bsd->fd', hidden_act, d_state, preferred_element_type=jnp.float32)
        d_act = jnp.einsum('bsd,fd->bsf', d_state, down_s[layer_idx], preferred_element_type=jnp.float32)
        _, gelu_pull = jax.vjp(gelu_tanh, pre_act)
        d_pre = gelu_pull(d_act)[0].astype(jnp.bfloat16)
        grad_up = jnp.einsum('bsd,bsf->df', normed, d_pre, preferred_element_type=jnp.float32)
        d_normed = jnp.einsum('bsf,df->bsd', d_pre, up_s[layer_idx], preferred_element_type=jnp.float32)
        grad_gain_mlp = jnp.sum(d_normed * unit_in, axis=(0, 1))
        if layer_idx > 0:
            grad_state = grad_state + rms_back(d_normed * gain_mlp[layer_idx], unit_in, inv_in)
        for grad_list, grad_val in zip(grad_lists, (grad_up, grad_down, grad_gain_mlp, grad_gain_proj, grad_proj)):
            grad_list.append(grad_val)
    stacked = tuple(jnp.stack(grad_list[::-1]) for grad_list in grad_lists)
    return (loss_part,) + stacked


def solution(mesh):
    model_n = mesh.shape['model']
    spec_list = (P('data', 'model', None), P(('data', 'model'), None, None), P(None, None, 'model'), P(None, 'model', None), P(), P(), P(), P(), P(), P())

    def distill_step(x_teach, x_stud, t_up, t_down, t_gain, s_up, s_down, s_gain_mlp, s_gain_proj, s_proj):
        n_feat = s_up.shape[0]
        loss_scale = 1.0 / (n_feat * x_teach.shape[0] * x_teach.shape[1] * x_teach.shape[2])

        def local_fn(teach_loc, stud_loc, up_loc, down_loc, gain_t, up_s, down_s, gain_mlp, gain_proj, proj_s):
            half_rows = stud_loc.shape[0] // 2
            seq_part = teach_loc.shape[1]
            teach_dim = teach_loc.shape[2]
            teach_view = teach_loc.reshape(model_n, 2, half_rows, seq_part, teach_dim)
            micro_outs = []
            for micro_idx in range(2):
                hidden = teach_view[:, micro_idx].reshape(model_n * half_rows, seq_part, teach_dim)
                feat_list = teacher_micro(hidden, up_loc, down_loc, gain_t, n_feat)
                row_feats = [feature_to_rows(feat_arr, model_n) for feat_arr in feat_list]
                x_rows = stud_loc[micro_idx * half_rows:(micro_idx + 1) * half_rows]
                micro_outs.append(student_micro(x_rows, row_feats, up_s, down_s, gain_mlp, gain_proj, proj_s, loss_scale))
            totals = tuple(first_mb + second_mb for first_mb, second_mb in zip(micro_outs[0], micro_outs[1]))
            return lax.psum(totals, ('data', 'model'))

        mapped = jax.shard_map(local_fn, mesh=mesh, in_specs=spec_list, out_specs=(P(),) * 6, check_vma=False)
        return mapped(x_teach, x_stud, t_up, t_down, t_gain, s_up, s_down, s_gain_mlp, s_gain_proj, s_proj)

    return distill_step
```

profile of v0, /device:TPU:1, one launch (start us, length us, event | category | flops | bytes accessed | tf_op | source)
XLA Modules:
  0.0 1222.7 jit_solution(6929998731979694374)
XLA Ops:
  25.9 6.4 reduce-scatter.49.cloned.1.call-done
  32.2 14.8 %reduce-scatter.97.cloned.1.call-done = bf16[2,64,768]{2,1,0:T(8,128)(2,1)} async-done(((bf16[2,128,768]{2,1,0:T(8,128)(2,1)}), bf16[2,64,768]{2,1,0:T(8,128)(2,1)}) %reduce-scatter.97.cloned.1.call-update) | async-done | bytes 196624 | tf_op jit(solution)/shard_map/reduce_scatter | solution.py:31
  68.2 14.6 %reduce-scatter.51.cloned.1.call-done = bf16[2,64,768]{2,1,0:T(8,128)(2,1)} async-done(((bf16[2,128,768]{2,1,0:T(8,128)(2,1)}), bf16[2,64,768]{2,1,0:T(8,128)(2,1)}) %reduce-scatter.51.cloned.1.call-update) | async-done | bytes 196624 | tf_op jit(solution)/shard_map/reduce_scatter | solution.py:31
  104.2 13.5 %reduce-scatter.53.cloned.1.call-done = bf16[2,64,768]{2,1,0:T(8,128)(2,1)} async-done(((bf16[2,128,768]{2,1,0:T(8,128)(2,1)}), bf16[2,64,768]{2,1,0:T(8,128)(2,1)}) %reduce-scatter.53.cloned.1.call-update) | async-done | bytes 196624 | tf_op jit(solution)/shard_map/reduce_scatter | solution.py:31
  140.7 13.1 %reduce-scatter.55.cloned.1.call-done = bf16[2,64,768]{2,1,0:T(8,128)(2,1)} async-done(((bf16[2,128,768]{2,1,0:T(8,128)(2,1)}), bf16[2,64,768]{2,1,0:T(8,128)(2,1)}) %reduce-scatter.55.cloned.1.call-update) | async-done | bytes 196624 | tf_op jit(solution)/shard_map/reduce_scatter | solution.py:31
  177.4 12.6 %reduce-scatter.57.cloned.1.call-done = bf16[2,64,768]{2,1,0:T(8,128)(2,1)} async-done(((bf16[2,128,768]{2,1,0:T(8,128)(2,1)}), bf16[2,64,768]{2,1,0:T(8,128)(2,1)}) %reduce-scatter.57.cloned.1.call-update) | async-done | bytes 196624 | tf_op jit(solution)/shard_map/reduce_scatter | solution.py:31
  212.6 13.4 %reduce-scatter.59.cloned.1.call-done = bf16[2,64,768]{2,1,0:T(8,128)(2,1)} async-done(((bf16[2,128,768]{2,1,0:T(8,128)(2,1)}), bf16[2,64,768]{2,1,0:T(8,128)(2,1)}) %reduce-scatter.59.cloned.1.call-update) | async-done | bytes 196624 | tf_op jit(solution)/shard_map/reduce_scatter | solution.py:31
  247.2 13.5 %reduce-scatter.61.cloned.1.call-done = bf16[2,64,768]{2,1,0:T(8,128)(2,1)} async-done(((bf16[2,128,768]{2,1,0:T(8,128)(2,1)}), bf16[2,64,768]{2,1,0:T(8,128)(2,1)}) %reduce-scatter.61.cloned.1.call-update) | async-done | bytes 196624 | tf_op jit(solution)/shard_map/reduce_scatter | solution.py:31
  282.9 13.5 %reduce-scatter.63.cloned.1.call-done = bf16[2,64,768]{2,1,0:T(8,128)(2,1)} async-done(((bf16[2,128,768]{2,1,0:T(8,128)(2,1)}), bf16[2,64,768]{2,1,0:T(8,128)(2,1)}) %reduce-scatter.63.cloned.1.call-update) | async-done | bytes 196624 | tf_op jit(solution)/shard_map/reduce_scatter | solution.py:31
  319.1 13.5 %reduce-scatter.65.cloned.1.call-done = bf16[2,64,768]{2,1,0:T(8,128)(2,1)} async-done(((bf16[2,128,768]{2,1,0:T(8,128)(2,1)}), bf16[2,64,768]{2,1,0:T(8,128)(2,1)}) %reduce-scatter.65.cloned.1.call-update) | async-done | bytes 196624 | tf_op jit(solution)/shard_map/reduce_scatter | solution.py:31
  355.0 13.5 %reduce-scatter.67.cloned.1.call-done = bf16[2,64,768]{2,1,0:T(8,128)(2,1)} async-done(((bf16[2,128,768]{2,1,0:T(8,128)(2,1)}), bf16[2,64,768]{2,1,0:T(8,128)(2,1)}) %reduce-scatter.67.cloned.1.call-update) | async-done | bytes 196624 | tf_op jit(solution)/shard_map/reduce_scatter | solution.py:31
  389.8 13.7 %reduce-scatter.69.cloned.1.call-done = bf16[2,64,768]{2,1,0:T(8,128)(2,1)} async-done(((bf16[2,128,768]{2,1,0:T(8,128)(2,1)}), bf16[2,64,768]{2,1,0:T(8,128)(2,1)}) %reduce-scatter.69.cloned.1.call-update) | async-done | bytes 196624 | tf_op jit(solution)/shard_map/reduce_scatter | solution.py:31
  426.4 12.9 %reduce-scatter.71.cloned.1.call-done = bf16[2,64,768]{2,1,0:T(8,128)(2,1)} async-done(((bf16[2,128,768]{2,1,0:T(8,128)(2,1)}), bf16[2,64,768]{2,1,0:T(8,128)(2,1)}) %reduce-scatter.71.cloned.1.call-update) | async-done | bytes 196624 | tf_op jit(solution)/shard_map/reduce_scatter | solution.py:31
  462.2 13.4 %reduce-scatter.73.cloned.1.call-done = bf16[2,64,768]{2,1,0:T(8,128)(2,1)} async-done(((bf16[2,128,768]{2,1,0:T(8,128)(2,1)}), bf16[2,64,768]{2,1,0:T(8,128)(2,1)}) %reduce-scatter.73.cloned.1.call-update) | async-done | bytes 196624 | tf_op jit(solution)/shard_map/reduce_scatter | solution.py:31
  498.2 13.5 %reduce-scatter.75.cloned.1.call-done = bf16[2,64,768]{2,1,0:T(8,128)(2,1)} async-done(((bf16[2,128,768]{2,1,0:T(8,128)(2,1)}), bf16[2,64,768]{2,1,0:T(8,128)(2,1)}) %reduce-scatter.75.cloned.1.call-update) | async-done | bytes 196624 | tf_op jit(solution)/shard_map/reduce_scatter | solution.py:31
  533.0 13.5 %reduce-scatter.77.cloned.1.call-done = bf16[2,64,768]{2,1,0:T(8,128)(2,1)} async-done(((bf16[2,128,768]{2,1,0:T(8,128)(2,1)}), bf16[2,64,768]{2,1,0:T(8,128)(2,1)}) %reduce-scatter.77.cloned.1.call-update) | async-done | bytes 196624 | tf_op jit(solution)/shard_map/reduce_scatter | solution.py:31
  570.2 12.2 reduce-scatter.79.cloned.1.call-done
  615.1 5.4 reduce-scatter.81.cloned.1.call-done
  683.3 9.7 reduce-scatter.85.cloned.1.call-done
  944.9 11.3 add.1596
  956.2 11.8 add.1595
  979.6 68.4 %all-reduce = (f32[]{:T(128)}, f32[6,312]{1,0:T(8,128)}, f32[6,312]{1,0:T(8,128)}) all-reduce(f32[]{:T(128)S(6)} %multiply.538, f32[6,312]{1,0:T(8,128)S(1)} %add.1597, f32[6,312]{1,0:T(8,128)S(1)} %add.1598), channel_id=1, replica_groups=mesh['data'=64,'model'=2] {'data','model'}, use_global_device_ids=true, to_apply=%region_122.0 | all-reduce | flops 3745 | bytes 29960 | tf_op jit(solution)/shard_map/psum | solution.py:110
  1048.1 150.3 %all-reduce.4.cloned.1.call-done = (f32[6,312,1248]{2,1,0:T(8,128)}, f32[6,1248,312]{1,2,0:T(8,128)}, f32[6,312,768]{2,1,0:T(8,128)}) async-done(((f32[6,312,1248]{2,1,0:T(8,128)}, f32[6,1248,312]{1,2,0:T(8,128)}, f32[6,312,768]{2,1,0:T(8,128)}), (f32[6,312,1248]{2,1,0:T(8,128)}, f32[6,1248,312]{1,2,0:T(8,128)}, f32[6,312,768]{2,1,0:T(8,128)})) %all-reduce.4.cloned.1.call-update) | async-done | bytes 24440848 | tf_op jit(solution)/shard_map/psum | solution.py:110
  1198.4 9.4 copy.67
  (935 shorter events, 709.0 us)
Async XLA Ops:
  25.8 42.4 %reduce-scatter.99.cloned.1.call-start = ((), (), s32[]{:S(2)}) async-start(), calls=%async_computation.85 | async-start | bytes 589824 | tf_op jit(solution)/shard_map/reduce_scatter | solution.py:31
  63.2 39.9 %reduce-scatter.101.cloned.1.call-start = ((), (), s32[]{:S(2)}) async-start(), calls=%async_computation.86 | async-start | bytes 589824 | tf_op jit(solution)/shard_map/reduce_scatter | solution.py:31
  98.0 41.0 %reduce-scatter.103.cloned.1.call-start = ((), (), s32[]{:S(2)}) async-start(), calls=%async_computation.87 | async-start | bytes 589824 | tf_op jit(solution)/shard_map/reduce_scatter | solution.py:31
  134.6 41.6 %reduce-scatter.105.cloned.1.call-start = ((), (), s32[]{:S(2)}) async-start(), calls=%async_computation.88 | async-start | bytes 589824 | tf_op jit(solution)/shard_map/reduce_scatter | solution.py:31
  171.9 39.4 %reduce-scatter.107.cloned.1.call-start = ((), (), s32[]{:S(2)}) async-start(), calls=%async_computation.89 | async-start | bytes 589824 | tf_op jit(solution)/shard_map/reduce_scatter | solution.py:31
  206.3 39.9 %reduce-scatter.109.cloned.1.call-start = ((), (), s32[]{:S(2)}) async-start(), calls=%async_computation.90 | async-start | bytes 589824 | tf_op jit(solution)/shard_map/reduce_scatter | solution.py:31
  241.1 40.7 %reduce-scatter.111.cloned.1.call-start = ((), (), s32[]{:S(2)}) async-start(), calls=%async_computation.91 | async-start | bytes 589824 | tf_op jit(solution)/shard_map/reduce_scatter | solution.py:31
  276.8 41.3 %reduce-scatter.113.cloned.1.call-start = ((), (), s32[]{:S(2)}) async-start(), calls=%async_computation.92 | async-start | bytes 589824 | tf_op jit(solution)/shard_map/reduce_scatter | solution.py:31
  313.2 40.8 %reduce-scatter.115.cloned.1.call-start = ((), (), s32[]{:S(2)}) async-start(), calls=%async_computation.93 | async-start | bytes 589824 | tf_op jit(solution)/shard_map/reduce_scatter | solution.py:31
  348.8 39.8 %reduce-scatter.117.cloned.1.call-start = ((), (), s32[]{:S(2)}) async-start(), calls=%async_computation.94 | async-start | bytes 589824 | tf_op jit(solution)/shard_map/reduce_scatter | solution.py:31
  383.6 41.1 %reduce-scatter.119.cloned.1.call-start = ((), (), s32[]{:S(2)}) async-start(), calls=%async_computation.95 | async-start | bytes 589824 | tf_op jit(solution)/shard_map/reduce_scatter | solution.py:31
  419.7 41.4 %reduce-scatter.121.cloned.1.call-start = ((), (), s32[]{:S(2)}) async-start(), calls=%async_computation.96 | async-start | bytes 589824 | tf_op jit(solution)/shard_map/reduce_scatter | solution.py:31
  456.0 41.0 %reduce-scatter.123.cloned.1.call-start = ((), (), s32[]{:S(2)}) async-start(), calls=%async_computation.97 | async-start | bytes 589824 | tf_op jit(solution)/shard_map/reduce_scatter | solution.py:31
  491.9 40.0 %reduce-scatter.125.cloned.1.call-start = ((), (), s32[]{:S(2)}) async-start(), calls=%async_computation.98 | async-start | bytes 589824 | tf_op jit(solution)/shard_map/reduce_scatter | solution.py:31
  526.9 41.6 %reduce-scatter.127.cloned.1.call-start = ((), (), s32[]{:S(2)}) async-start(), calls=%async_computation.99 | async-start | bytes 589824 | tf_op jit(solution)/shard_map/reduce_scatter | solution.py:31
  568.5 44.9 %reduce-scatter.129.cloned.1.call-start = ((), (), s32[]{:S(2)}) async-start(), calls=%async_computation.100 | async-start | bytes 589824 | tf_op jit(solution)/shard_map/reduce_scatter | solution.py:31
  608.4 46.1 %reduce-scatter.131.cloned.1.call-start = ((), (), s32[]{:S(2)}) async-start(), calls=%async_computation.101 | async-start | bytes 589824 | tf_op jit(solution)/shard_map/reduce_scatter | solution.py:31
  647.5 30.0 %all-to-all-start.1 = ((bf16[2,1,64,768]{3,2,1,0:T(8,128)(2,1)}), bf16[2,1,64,768]{3,2,1,0:T(8,128)(2,1)}, u32[]{:S(2)}, u32[]{:S(2)}) async-start(bf16[2,1,64,768]{3,2,1,0:T(8,128)(2,1)} %bitcast.51), calls=%async_computation.9 | async-start | bytes 393216 | tf_op jit(solution)/shard_map/all_to_all | solution.py:41
  677.5 46.8 %reduce-scatter.135.cloned.1.call-start = ((), (), s32[]{:S(2)}) async-start(), calls=%async_computation.103 | async-start | bytes 589824 | tf_op jit(solution)/shard_map/reduce_scatter | solution.py:31
  720.2 39.0 %reduce-scatter.137.cloned.1.call-start = ((), (), s32[]{:S(2)}) async-start(), calls=%async_computation.104 | async-start | bytes 589824 | tf_op jit(solution)/shard_map/reduce_scatter | solution.py:31
  759.2 37.3 %reduce-scatter.139.cloned.1.call-start = ((), (), s32[]{:S(2)}) async-start(), calls=%async_computation.105 | async-start | bytes 589824 | tf_op jit(solution)/shard_map/reduce_scatter | solution.py:31
  791.0 47.1 %reduce-scatter.141.cloned.1.call-start = ((), (), s32[]{:S(2)}) async-start(), calls=%async_computation.106 | async-start | bytes 589824 | tf_op jit(solution)/shard_map/reduce_scatter | solution.py:31
  835.3 31.3 %reduce-scatter.95.cloned.1.call-start = ((), (), s32[]{:S(2)}) async-start(), calls=%async_computation.83 | async-start | bytes 589824 | tf_op jit(solution)/shard_map/reduce_scatter | solution.py:31
  881.9 316.5 %all-reduce.4.cloned.1.call-start = ((), (), s32[]{:S(2)}) async-start(), calls=%async_computation.108 | async-start | bytes 49840128 | tf_op jit(solution)/shard_map/psum | solution.py:110
  (225 other events, 3816.4 us)
Sparse Core Ops, SparseCore 0:
  19.0 13.1 reduce-scatter.48
  35.2 11.7 reduce-scatter.96
  56.4 11.7 reduce-scatter.98
  71.0 11.7 reduce-scatter.50
  91.2 11.7 reduce-scatter.100
  105.9 11.7 reduce-scatter.52
  127.1 11.7 reduce-scatter.102
  163.6 11.7 reduce-scatter.104
  199.5 11.7 reduce-scatter.106
  214.1 11.7 reduce-scatter.58
  234.3 11.7 reduce-scatter.108
  449.2 11.7 reduce-scatter.120
  485.2 11.7 reduce-scatter.122
  534.7 11.7 reduce-scatter.76
  593.1 11.9 reduce-scatter.128
  608.5 11.9 reduce-scatter.80
  702.8 11.8 reduce-scatter.134
  739.5 11.8 reduce-scatter.136
  753.8 11.8 reduce-scatter.88
  775.8 11.9 reduce-scatter.138
  791.1 12.0 reduce-scatter.90
  813.9 11.8 reduce-scatter.140
  850.0 11.8 reduce-scatter.94
  968.4 229.9 all-reduce.3
  (25 shorter events, 293.6 us)
where the time goes:
time: 1240 us; the launch traced here: 1220 us
  waiting for transfers between devices  426 us (34%)
  matrix products  381 us (31%)
  blocking collectives  188 us (15%)
  other arithmetic  125 us (10%)
  starting transfers between devices  46.1 us (4%)
  local copies, waits for them, and re-layouts  31.4 us (3%)
  between operations  25.7 us (2%)
    reduce_scatter x48, waiting for transfers between devices, teacher_micro(): lax.psum_scatter(part_out, 'model', scatter_dimension=1, tiled=True)  275 us
    dot_general x48, matrix products, teacher_micro(): jnp.einsum('bsf,fd->bsd', hidden_act, down_loc[layer_idx], preferred_elem...  228 us
    psum x1, waiting for transfers between devices, local_fn(): return lax.psum(totals, ('data', 'model'))  150 us
    all_gather x48, blocking collectives, teacher_micro(): gathered = lax.all_gather(normed, 'model', axis=1, tiled=True)  111 us
    psum x1, blocking collectives, local_fn(): return lax.psum(totals, ('data', 'model'))  68.4 us
    reduce_sum x46, other arithmetic, rms_scale(): jnp.mean(widened * widened, axis=-1, keepdims=True) + NORM_EPS  58.1 us
    all_to_all x10, starting transfers between devices, feature_to_rows(): moved_rows = lax.all_to_all(grouped, 'model', 0, 2, tiled=True)  43 us
    dot_general x12, matrix products, student_micro(): jnp.einsum('bsd,dk->bsk', projected, proj_s[layer_idx], preferred_element...  30 us
  transfers between devices with their start and end apart: 59, of which 37 were waited for; matrix products, arithmetic and copies ran while one was open for 24% of the time, Pallas kernels for 0%

commit v1 on v0

v1 whole, which is shorter than its diff:
```python
import functools
import jax
import jax.numpy as jnp
from jax import lax
from jax.experimental import pallas as pl
from jax.experimental.pallas import tpu as pltpu
from jax.sharding import PartitionSpec as P

NORM_EPS = 1e-6
GELU_K = 0.7978845608028654
GELU_C = 0.044715
MESH = pl.DeviceIdType.MESH
BF = jnp.bfloat16
F32 = jnp.float32


def gelu(x):
    x2 = x * x
    t = jnp.tanh(x * (GELU_K + (GELU_K * GELU_C) * x2))
    hx = 0.5 * x
    return hx + hx * t


def gelu_grad(x):
    x2 = x * x
    t = jnp.tanh(x * (GELU_K + (GELU_K * GELU_C) * x2))
    inner = GELU_K + (3.0 * GELU_K * GELU_C) * x2
    return 0.5 * (1.0 + t) + (0.5 * x) * (1.0 - t * t) * inner


def inv_rms(w):
    return lax.rsqrt(jnp.mean(w * w, axis=-1, keepdims=True) + NORM_EPS)


def dot(a, b):
    return jnp.dot(a, b, preferred_element_type=F32)


def dot_tn(a, b):
    return lax.dot_general(a, b, (((0,), (0,)), ((), ())), preferred_element_type=F32)


def dot_nt(a, b):
    return lax.dot_general(a, b, (((1,), (1,)), ((), ())), preferred_element_type=F32)


def teacher_kernel(per_feat, x_ref, gain_ref, up_hbm, down_hbm, feat_ref, h, a, u, own, peer, upb, downb, wsem, xsem, ssem, rsem):
    core = lax.axis_index('model')
    other = 1 - core
    n_layers = up_hbm.shape[0]
    n_chunk, rows, dim = h.shape
    ff = upb.shape[2]
    half = x_ref.shape[1]
    sub = 32

    def up_copy(layer, slot):
        return pltpu.make_async_copy(up_hbm.at[layer], upb.at[slot], wsem.at[slot, 0])

    def down_copy(layer, slot):
        return pltpu.make_async_copy(down_hbm.at[layer], downb.at[slot], wsem.at[slot, 1])

    def exchange(chunk, slot):
        return pltpu.make_async_remote_copy(
            src_ref=own.at[chunk], dst_ref=peer.at[slot, chunk], send_sem=ssem.at[chunk], recv_sem=rsem.at[slot, chunk],
            device_id={'model': other}, device_id_type=MESH)

    up_copy(0, 0).start()
    down_copy(0, 0).start()
    barrier = pltpu.get_barrier_semaphore()
    pl.semaphore_signal(barrier, inc=1, device_id={'model': other}, device_id_type=MESH)
    pl.semaphore_wait(barrier, 1)
    mine = pl.ds(pl.multiple_of(core * half, half), half)
    x_copy = pltpu.make_async_remote_copy(
        src_ref=x_ref, dst_ref=h.at[:, mine, :], send_sem=xsem.at[0], recv_sem=xsem.at[1],
        device_id={'model': other}, device_id_type=MESH)
    x_copy.start()
    h[:, mine, :] = x_ref[...]
    own[...] = jnp.zeros_like(own)
    peer[1] = jnp.zeros(peer.shape[1:], BF)

    def combine(chunk, slot, gain_row):
        for r in range(0, rows, sub):
            sl = pl.ds(r, sub)
            w = h[chunk, sl, :].astype(F32) + (own[chunk, sl, :].astype(F32) + peer[slot, chunk, sl, :].astype(F32))
            hb = w.astype(BF)
            h[chunk, sl, :] = hb
            w = hb.astype(F32)
            a[chunk, sl, :] = (w * inv_rms(w) * gain_row).astype(BF)

    x_copy.wait()
    combine(0, 1, gain_ref[pl.ds(0, 1), :])

    def keep(layer, chunk):
        @pl.when((lax.rem(layer + 1, per_feat) == 0) & (core == chunk // 2))
        def _():
            feat_ref[layer // per_feat, chunk % 2] = h[chunk]

    def layer_step(layer, carry):
        slot = lax.rem(layer, 2)
        prev = 1 - slot

        @pl.when(layer + 1 < n_layers)
        def _():
            up_copy(layer + 1, prev).start()
            down_copy(layer + 1, prev).start()

        up_copy(layer, slot).wait()
        down_copy(layer, slot).wait()
        for chunk in range(n_chunk):
            nxt = (chunk + 1) % n_chunk
            if nxt:
                @pl.when(layer > 0)
                def _():
                    exchange(nxt, prev).wait()
                src, gain_at = prev, layer
            else:
                exchange(nxt, slot).wait()
                src, gain_at = slot, jnp.minimum(layer + 1, n_layers - 1)
            gain_row = gain_ref[pl.ds(gain_at, 1), :]
            act = a[chunk]
            for n in range(0, ff, 512):
                u[chunk % 2, :, n:n + 512] = gelu(dot(act, upb[slot, :, n:n + 512])).astype(BF)
            own[chunk] = dot(u[chunk % 2], downb[slot]).astype(BF)
            combine(nxt, src, gain_row)
            exchange(chunk, slot).start()
            if nxt:
                @pl.when(layer > 0)
                def _():
                    keep(layer - 1, nxt)
            else:
                keep(layer, nxt)
        return carry

    lax.fori_loop(0, n_layers, layer_step, 0)
    last = (n_layers - 1) % 2
    for chunk in range(1, n_chunk):
        exchange(chunk, last).wait()
        combine(chunk, last, gain_ref[pl.ds(0, 1), :])
        keep(n_layers - 1, chunk)


def teacher(x_loc, up_loc, down_loc, gain, n_feat):
    n_chunk, half, dim = x_loc.shape
    n_layers, _, ff = up_loc.shape
    rows = 2 * half
    flops = 4 * n_layers * n_chunk * rows * dim * ff
    vmem = pl.BlockSpec(memory_space=pltpu.VMEM)
    hbm = pl.BlockSpec(memory_space=pl.ANY)
    return pl.pallas_call(
        functools.partial(teacher_kernel, n_layers // n_feat),
        out_shape=jax.ShapeDtypeStruct((n_feat, n_chunk // 2, rows, dim), BF),
        in_specs=[vmem, vmem, hbm, hbm],
        out_specs=vmem,
        scratch_shapes=[
            pltpu.VMEM((n_chunk, rows, dim), BF),
            pltpu.VMEM((n_chunk, rows, dim), BF),
            pltpu.VMEM((2, rows, ff), BF),
            pltpu.VMEM((n_chunk, rows, dim), BF),
            pltpu.VMEM((2, n_chunk, rows, dim), BF),
            pltpu.VMEM((2, dim, ff), BF),
            pltpu.VMEM((2, ff, dim), BF),
            pltpu.SemaphoreType.DMA((2, 2)),
            pltpu.SemaphoreType.DMA((2,)),
            pltpu.SemaphoreType.DMA((n_chunk,)),
            pltpu.SemaphoreType.DMA((2, n_chunk)),
        ],
        compiler_params=pltpu.CompilerParams(collective_id=0, has_side_effects=True, vmem_limit_bytes=60 * 1024 * 1024),
        cost_estimate=pl.CostEstimate(flops=flops, bytes_accessed=2 * n_layers * dim * ff * 2, transcendentals=n_layers * n_chunk * rows * ff),
        name='teacher',
    )(x_loc, gain, up_loc, down_loc)


def student_kernel(loss_scale, x_ref, gm_ref, gp_ref, feat_hbm, up_hbm, down_hbm, proj_hbm, gup_hbm, gdown_hbm, gproj_hbm, small_ref,
                   st, nm, ha, pj, de, pre, gs, upb, downb, projb, featb, gub, gdb, gpb, wsem, osem):
    n_layers, dim, ff = up_hbm.shape
    tdim = proj_hbm.shape[2]
    cuts = [(n, min(n + 512, ff)) for n in range(0, ff, 512)]

    def loads(j):
        return [pltpu.make_async_copy(src.at[j], dst.at[j], wsem.at[j, i])
                for i, (src, dst) in enumerate(((up_hbm, upb), (down_hbm, downb), (proj_hbm, projb), (feat_hbm, featb)))]

    def stores(j, slot):
        return [pltpu.make_async_copy(src.at[slot], dst.at[j], osem.at[slot, i])
                for i, (src, dst) in enumerate(((gpb, gproj_hbm), (gdb, gdown_hbm), (gub, gup_hbm)))]

    for j in range(n_layers):
        for cp in loads(j):
            cp.start()
    for r in range(x_ref.shape[0]):
        st[0, r * x_ref.shape[2]:(r + 1) * x_ref.shape[2], :] = x_ref[r].astype(F32).T.astype(BF)
    small_ref[...] = jnp.zeros_like(small_ref)

    def fwd(j, carry):
        for cp in loads(j):
            cp.wait()
        w = st[j].astype(F32)
        normed = (w * inv_rms(w) * gm_ref[pl.ds(j, 1), :]).astype(BF)
        nm[j] = normed
        for lo, hi in cuts:
            p = dot(normed, upb[j, :, lo:hi])
            pre[j, :, lo:hi] = p
            ha[j, :, lo:hi] = gelu(p).astype(BF)
        s1 = (w + dot_nt(ha[j], downb[j])).astype(BF)
        st[j + 1] = s1
        w1 = s1.astype(F32)
        projected = (w1 * inv_rms(w1) * gp_ref[pl.ds(j, 1), :]).astype(BF)
        pj[j] = projected
        for lo in range(0, tdim, 256):
            hi = lo + 256
            e = dot(projected, projb[j, :, lo:hi]) - featb[j, :, lo:hi].astype(F32)
            small_ref[pl.ds(12, 1), lo:hi] += jnp.sum(e * e, axis=0, keepdims=True) * loss_scale
            de[j, :, lo:hi] = ((2.0 * loss_scale) * e).astype(BF)
        return carry

    lax.fori_loop(0, n_layers, fwd, 0)
    gs[...] = jnp.zeros_like(gs)

    def bwd(i, carry):
        j = n_layers - 1 - i
        slot = lax.rem(i, 2)

        @pl.when(i >= 2)
        def _():
            for cp in stores(j, slot):
                cp.wait()
        st_proj, st_down, st_up = stores(j, slot)
        d_err = de[j]
        d_projected = dot_nt(d_err, projb[j])
        gpb[slot] = dot_tn(pj[j], d_err)
        w1 = st[j + 1].astype(F32)
        inv1 = inv_rms(w1)
        unit1 = w1 * inv1
        small_ref[pl.ds(6 + j, 1), 0:dim] = jnp.sum(d_projected * unit1, axis=0, keepdims=True)
        gu = d_projected * gp_ref[pl.ds(j, 1), :]
        g = gs[...] + inv1 * (gu - unit1 * jnp.mean(gu * unit1, axis=-1, keepdims=True))
        d_state = g.astype(BF)
        st_proj.start()
        for lo, hi in cuts:
            d_act = dot(d_state, downb[j, :, lo:hi])
            ha_cut = ha[j, :, lo:hi]
            d_pre = (gelu_grad(pre[j, :, lo:hi]) * d_act).astype(BF)
            gdb[slot, :, lo:hi] = dot_tn(d_state, ha_cut)
            ha[j, :, lo:hi] = d_pre
        st_down.start()
        d_normed = dot_nt(ha[j], upb[j])
        for lo, hi in cuts:
            gub[slot, :, lo:hi] = dot_tn(nm[j], ha[j, :, lo:hi])
        st_up.start()
        w = st[j].astype(F32)
        inv0 = inv_rms(w)
        unit0 = w * inv0
        small_ref[pl.ds(j, 1), 0:dim] = jnp.sum(d_normed * unit0, axis=0, keepdims=True)
        gu = d_normed * gm_ref[pl.ds(j, 1), :]
        gs[...] = g + inv0 * (gu - unit0 * jnp.mean(gu * unit0, axis=-1, keepdims=True))
        return carry

    lax.fori_loop(0, n_layers, bwd, 0)
    for slot in range(2):
        for cp in stores(0, slot):
            cp.wait()


def student(x, feats, up_s, down_s, gm, gp, proj_s, loss_scale):
    n_layers, dim, ff = up_s.shape
    tokens = x.shape[0] * x.shape[2]
    tdim = proj_s.shape[2]
    vmem = pl.BlockSpec(memory_space=pltpu.VMEM)
    hbm = pl.BlockSpec(memory_space=pl.ANY)
    flops = 6 * tokens * n_layers * dim * (2 * ff + tdim)
    return pl.pallas_call(
        functools.partial(student_kernel, loss_scale),
        out_shape=(
            jax.ShapeDtypeStruct(up_s.shape, F32),
            jax.ShapeDtypeStruct(down_s.shape, F32),
            jax.ShapeDtypeStruct(proj_s.shape, F32),
            jax.ShapeDtypeStruct((16, tdim), F32),
        ),
        in_specs=[vmem, vmem, vmem, hbm, hbm, hbm, hbm],
        out_specs=(hbm, hbm, hbm, vmem),
        scratch_shapes=[
            pltpu.VMEM((n_layers + 1, tokens, dim), BF),
            pltpu.VMEM((n_layers, tokens, dim), BF),
            pltpu.VMEM((n_layers, tokens, ff), BF),
            pltpu.VMEM((n_layers, tokens, dim), BF),
            pltpu.VMEM((n_layers, tokens, tdim), BF),
            pltpu.VMEM((n_layers, tokens, ff), F32),
            pltpu.VMEM((tokens, dim), F32),
            pltpu.VMEM(up_s.shape, BF),
            pltpu.VMEM(down_s.shape, BF),
            pltpu.VMEM(proj_s.shape, BF),
            pltpu.VMEM((n_layers, tokens, tdim), BF),
            pltpu.VMEM((2,) + up_s.shape[1:], F32),
            pltpu.VMEM((2,) + down_s.shape[1:], F32),
            pltpu.VMEM((2,) + proj_s.shape[1:], F32),
            pltpu.SemaphoreType.DMA((n_layers, 4)),
            pltpu.SemaphoreType.DMA((2, 3)),
        ],
        compiler_params=pltpu.CompilerParams(vmem_limit_bytes=60 * 1024 * 1024),
        cost_estimate=pl.CostEstimate(flops=flops, bytes_accessed=40 * 1024 * 1024, transcendentals=2 * n_layers * tokens * ff),
        name='student',
    )(x, gm, gp, feats, up_s, down_s, proj_s)


def solution(mesh):
    spec_list = (P('data', 'model', None), P(('data', 'model'), None, None), P(None, None, 'model'), P(None, 'model', None), P(), P(), P(), P(), P(), P())

    def distill_step(x_teach, x_stud, t_up, t_down, t_gain, s_up, s_down, s_gain_mlp, s_gain_proj, s_proj):
        n_feat = s_up.shape[0]
        loss_scale = 1.0 / (n_feat * x_teach.shape[0] * x_teach.shape[1] * x_teach.shape[2])

        def local_fn(teach_loc, stud_loc, up_loc, down_loc, gain_t, up_s, down_s, gain_mlp, gain_proj, proj_s):
            dim = stud_loc.shape[2]
            tokens = stud_loc.shape[0] * stud_loc.shape[1]
            feats = teacher(teach_loc, up_loc, down_loc, gain_t, n_feat).reshape(n_feat, tokens, -1)
            g_up, g_down, g_proj, small = student(jnp.swapaxes(stud_loc, 1, 2), feats, up_s, jnp.swapaxes(down_s, 1, 2), gain_mlp, gain_proj, proj_s, loss_scale)
            g_up, g_down, g_proj, small = lax.psum((g_up, g_down, g_proj, small), ('data', 'model'))
            return jnp.sum(small[12]), g_up, jnp.swapaxes(g_down, 1, 2), small[0:6, :dim], small[6:12, :dim], g_proj

        mapped = jax.shard_map(local_fn, mesh=mesh, in_specs=spec_list, out_specs=(P(),) * 6, check_vma=False)
        return mapped(x_teach, x_stud, t_up, t_down, t_gain, s_up, s_down, s_gain_mlp, s_gain_proj, s_proj)

    return distill_step
```

time: 1240 us -> 389 us (0.31); the launches traced: 1220 us -> 389 us
  matrix products: 381 us -> 0 us
  waiting for transfers between devices: 426 us -> 160 us
  Pallas kernels: 0 us -> 126 us
  other arithmetic: 125 us -> 0.61 us
  blocking collectives: 188 us -> 69.6 us
  starting transfers between devices: 46.1 us -> 0.04 us
  local copies, waits for them, and re-layouts: 31.4 us -> 18.4 us
    dot_general x156 -> x0, matrix products: 381 us -> none  [the longest x48 228 us: teacher_micro(): jnp.einsum('bsf,fd->bsd', hidden_act, down_loc[layer_idx], preferred_elem...]
    reduce_scatter x48 -> x0, waiting for transfers between devices: 275 us -> none  [teacher_micro(): lax.psum_scatter(part_out, 'model', scatter_dimension=1, tiled=True)]
    pallas_call x0 -> x2, Pallas kernels: none -> 126 us  [the longest x1 99.6 us: teacher(): pl.pallas_call(functools.partial(teacher_kernel, n_layers // n_feat), out...]
    all_gather x48 -> x0, blocking collectives: 111 us -> none  [teacher_micro(): gathered = lax.all_gather(normed, 'model', axis=1, tiled=True)]
    reduce_sum x46 -> x1, other arithmetic: 58.1 us -> 0.6 us  [local_fn(): jnp.sum(small[12])]
    all_to_all x10 -> x0, starting transfers between devices: 43 us -> none  [feature_to_rows(): moved_rows = lax.all_to_all(grouped, 'model', 0, 2, tiled=True)]
    convert_element_type x25 -> x0, other arithmetic: 29.9 us -> none  [the longest x24 29.7 us: teacher_micro(): normed = (widened * inv_rms * gain_t[layer_idx]).astype(jnp.bfloat16)]
    add x9 -> x0, other arithmetic: 27.1 us -> none  [the longest x5 26.4 us: local_fn(): first_mb + second_mb]
  transfers between devices with their start and end apart: 59 -> 1, of which waited for: 37 -> 1; matrix products, arithmetic and copies ran while one was open for 24% -> 0% of each run, Pallas kernels for 0% -> 0%
where the time goes in v1:
time: 389 us
  waiting for transfers between devices  160 us (41%)
  Pallas kernels  126 us (32%)
  blocking collectives  69.6 us (18%)
  local copies, waits for them, and re-layouts  18.4 us (5%)
  between operations  14.1 us (4%)
    psum x1, waiting for transfers between devices, local_fn(): lax.psum((g_up, g_down, g_proj, small), ('data', 'model'))  160 us
    pallas_call x1, Pallas kernels, teacher(): pl.pallas_call(functools.partial(teacher_kernel, n_layers // n_feat), out...  99.6 us
    psum x1, blocking collectives, local_fn(): lax.psum((g_up, g_down, g_proj, small), ('data', 'model'))  69.6 us
    pallas_call x1, Pallas kernels, student(): pl.pallas_call(functools.partial(student_kernel, loss_scale), out_shape=(...  26.7 us
    unnamed x11, local copies, waits for them, and re-layouts  17.8 us
  transfers between devices with their start and end apart: 1, of which 1 were waited for; matrix products, arithmetic and copies ran while one was open for 0% of the time, Pallas kernels for 0%

profile of v1, /device:TPU:1, one launch (start us, length us, event | category | flops | bytes accessed | tf_op | source)
XLA Modules:
  0.0 388.8 jit_solution(16938471757626786645)
XLA Ops:
  7.2 0.0 all-reduce.3.cloned.1.call-start
  7.2 99.6 %teacher.1 = bf16[6,2,128,768]{3,2,1,0:T(8,128)(2,1)} custom-call(bf16[4,64,768]{2,1,0:T(8,128)(2,1)} %x_ref.1, f32[24,768]{1,0:T(8,128)} %gain_ref.1, bf16[24,768,1536]{2,1,0:T(8,128)(2,1)} %up_hbm.2, bf16[24,1536,768]{2,1,0:T(8,128)(2,1)} %down_hbm.1), custom_call_target="tpu_custom_call" | custom-call | flops 57982058496 | bytes 113246208 | tf_op jit(solution)/shard_map/teacher/pallas_call | solution.py:149
  106.8 26.7 %student.1 = (f32[6,312,1248]{2,1,0:T(8,128)}, f32[6,312,1248]{2,1,0:T(8,128)}, f32[6,312,768]{2,1,0:T(8,128)}, f32[16,768]{1,0:T(8,128)}) custom-call(bf16[2,312,128]{2,1,0:T(8,128)(2,1)} %bitcast.8, f32[6,312]{1,0:T(8,128)} %gm_ref.1, f32[6,312]{1,0:T(8,128)} %gp_ref.1, bf16[6,256,768]{2,1,0:T(8,128)(2,1)} %bitcast.9, bf16[6,312,1248]{2,1,0:T(8,128)(2,1)} %up_hbm.3, ...), custom_call_target="tpu_custom_call" | custom-call | flops 9385279488 | bytes 41943040 | tf_op jit(solution)/shard_map/student/pallas_call | solution.py:271
  133.5 0.0 copy-start.1
  133.5 0.0 all-reduce.3.cloned.1.call-update
  133.5 0.8 copy-done.1
  134.3 69.6 %psum.28 = f32[16,768]{1,0:T(8,128)S(1)} all-reduce(f32[16,768]{1,0:T(8,128)S(1)} %copy-done.1), channel_id=1, replica_groups=mesh['data'=64,'model'=2] {'data','model'}, use_global_device_ids=true, to_apply=%region_0.0 | all-reduce | flops 12288 | bytes 98304 | tf_op jit(solution)/shard_map/psum | solution.py:317
  203.9 0.6 slice_reduce_fusion
  204.6 0.6 fusion
  205.2 159.7 %all-reduce.3.cloned.1.call-done = (f32[6,312,1248]{2,1,0:T(8,128)}, f32[6,1248,312]{1,2,0:T(8,128)}, f32[6,312,768]{2,1,0:T(8,128)}) async-done(((f32[6,312,1248]{2,1,0:T(8,128)}, f32[6,1248,312]{1,2,0:T(8,128)}, f32[6,312,768]{2,1,0:T(8,128)}), (f32[6,312,1248]{2,1,0:T(8,128)}, f32[6,1248,312]{1,2,0:T(8,128)}, f32[6,312,768]{2,1,0:T(8,128)})) %all-reduce.3.cloned.1.call-update) | async-done | bytes 24440848 | tf_op jit(solution)/shard_map/psum | solution.py:317
  364.9 0.0 copy-start
  364.9 0.0 slice-start
  364.9 9.4 %copy.19 = f32[6,312,1248]{2,1,0:T(8,128)} copy(f32[6,312,1248]{2,1,0:T(8,128)} %get-tuple-element.20) | data formatting | bytes 18690048
  374.3 0.0 copy-done
  374.3 0.0 slice-start.1
  374.3 4.6 %copy.20 = f32[6,1248,312]{1,2,0:T(8,128)} copy(f32[6,1248,312]{1,2,0:T(8,128)S(1)} %copy-done) | data formatting | bytes 18690048
  378.9 0.0 slice-done
  378.9 0.5 slice-done.1
  379.4 2.5 copy.21
  (1 shorter events, 0.0 us)
Async XLA Ops:
  7.2 357.7 %all-reduce.3.cloned.1.call-start = ((), (), s32[]{:S(2)}) async-start(), calls=%async_computation | async-start | bytes 49840128 | tf_op jit(solution)/shard_map/psum | solution.py:317
  133.5 0.8 copy-start.1
  364.9 9.4 %copy-start = (f32[6,1248,312]{1,2,0:T(8,128)S(1)}, f32[6,1248,312]{1,2,0:T(8,128)}, u32[]{:S(2)}) copy-start(f32[6,1248,312]{1,2,0:T(8,128)} %get-tuple-element.21) | copy-start | bytes 28035076
  364.9 14.0 %slice-start = ((s8[5750784]{0:T(1024)(128)(4,1)}), s8[4194304]{0:T(1024)(128)(4,1)S(1)}, s32[]{:S(2)}) async-start(s8[5750784]{0:T(1024)(128)(4,1)} %bitcast.5), calls=%async_computation.1 | async-start | bytes 8388608
  374.3 5.1 %slice-start.1 = ((s8[5750784]{0:T(1024)(128)(4,1)}), s8[1556480]{0:T(1024)(128)(4,1)S(1)}, s32[]{:S(2)}) async-start(s8[5750784]{0:T(1024)(128)(4,1)} %bitcast.5), calls=%async_computation.2 | async-start | bytes 3112960
Sparse Core Ops, SparseCore 0:
  133.7 231.2 all-reduce.2
